TPU v7x, 32 devices: a whole 2x2x4 slice. The times are simulated.
32 devices in a mesh: rows: 4 (over y, x), wide: 8 (over z, core).
Axes of the slice: x: 2, y: 2, z: 4, core: 2. Of those that a mesh axis runs over, the one named last changes fastest.
Arguments:
- tokens: bfloat16 [16, 1024, 1024], P('rows', 'wide'), may hold values from -6 to 6
- segments: int32 [16, 1024], P('rows'), may hold values from 0 to 15, never falling along the last dimension, each value on 1 to 128 neighbouring positions
- w_qkv: bfloat16 [2, 1024, 3072], replicated, may hold values from -0.1875 to 0.1875
- b_qkv: float32 [2, 3072], replicated, may hold values from -3 to 3
- w_out: bfloat16 [2, 1024, 1024], replicated, may hold values from -1 to 1
- b_out: float32 [2, 1024], replicated, may hold values from -3 to 3
- norm_gain: float32 [2, 2, 1024], replicated, may hold values from 0.5 to 1.5
- norm_bias: float32 [2, 2, 1024], replicated, may hold values from -2 to 2
- w_up: bfloat16 [2, 4096, 1024], P(None, 'wide'), may hold values from -0.1875 to 0.1875
- b_up: bfloat16 [2, 4096], P(None, 'wide'), may hold values from -3 to 3
- w_down: bfloat16 [2, 4096, 1024], P(None, 'wide'), may hold values from -0.09375 to 0.09375
- b_down: float32 [2, 1024], replicated, may hold values from -2 to 2
- prefix: bfloat16 [2, 2, 64, 1024], replicated, may hold values from -6 to 6
- cotangent: bfloat16 [16, 1024, 1024], P('rows', 'wide'), may hold values from -6 to 6
Outputs:
- output: bfloat16 [16, 1024, 1024], P('rows', 'wide')
- grad_tokens: float32 [16, 1024, 1024], P('rows', 'wide')
- grad_prefix: float32 [2, 2, 64, 1024], replicated
Inputs may be any that keep to these rules, and one draw needn't show every extreme that they name: `segments`: along each row the pair ids never fall, each pair covers 1 to 128 consecutive positions, and some pair covers exactly 128.
All inputs are finite; a program needn't handle non-finite values.
Results may differ from a plain program's by a relative error of at most 0.02.
Values may be sent and summed in bfloat16 or wider, within the bound.
A program may use at most 320 MiB of HBM per device.

v0:
```python
import math
import jax
import jax.numpy as jnp
from jax import lax
from jax.sharding import PartitionSpec as P

HEADS = 16
PAIR_MAX = 128
LAYERS = 2


def extended(block, sides, width):
    for axis, dim in sides:
        count = lax.axis_size(axis)
        forward = [(i, i + 1) for i in range(count - 1)]
        backward = [(target, source) for source, target in forward]
        low = lax.ppermute(
            lax.slice_in_dim(block, block.shape[dim] - width, None, axis=dim), axis, forward
        )
        high = lax.ppermute(lax.slice_in_dim(block, 0, width, axis=dim), axis, backward)
        block = jnp.concatenate([low, block, high], axis=dim)
    return block


def normalize(values, gain, shift):
    center = values - jnp.mean(values, axis=-1, keepdims=True)
    spread = jnp.mean(center * center, axis=-1, keepdims=True)
    return center * lax.rsqrt(spread + 1e-05) * gain + shift


def gelu_exact(values):
    return jax.nn.gelu(values, approximate=False)


def gelu_back(pre_values, grad_values):
    return jax.vjp(gelu_exact, pre_values)[1](grad_values)[0]


def norm_grad(values, gain, shift, grad_values):
    return jax.vjp(lambda inner: normalize(inner, gain, shift), values)[1](grad_values)[0]


def multiply(left, right):
    return jnp.dot(left, right, preferred_element_type=jnp.float32)


def multiply_back(left, right):
    return lax.dot_general(
        left, right, (((1,), (1,)), ((), ())), preferred_element_type=jnp.float32
    )


def local(
    tokens,
    segments,
    w_qkv,
    b_qkv,
    w_out,
    b_out,
    norm_gain,
    norm_bias,
    w_up,
    b_up,
    w_down,
    b_down,
    prefix,
    cotangent,
):
    seqs_here, tok_here, model_width = tokens.shape
    rows_here = seqs_here * tok_here
    head_count = HEADS
    head_size = model_width // head_count
    score_scale = 1.0 / math.sqrt(head_size)
    rim_rows = PAIR_MAX
    prefix_len = prefix.shape[2]
    position = lax.axis_index("wide") * tok_here
    padded_ids = jnp.pad(segments, ((0, 0), (rim_rows, rim_rows)), constant_values=-1)
    query_ids = lax.dynamic_slice_in_dim(segments, position, tok_here, 1)
    window_ids = lax.dynamic_slice_in_dim(padded_ids, position, tok_here + 2 * rim_rows, 1)
    prefix_mask = jnp.ones((seqs_here, prefix_len, tok_here), dtype=bool)
    visible = jnp.concatenate(
        [prefix_mask, window_ids[:, :, None] == query_ids[:, None, :]], axis=1
    )[:, None]

    def split_heads(values):
        return values.reshape(seqs_here, values.shape[1], head_count, head_size)

    def with_prefix(layer_index, member, window_part):
        fixed_rows = jnp.broadcast_to(
            prefix[layer_index, member][None], (seqs_here, prefix_len, model_width)
        )
        return split_heads(jnp.concatenate([fixed_rows, window_part], axis=1))

    def score_block(queries, key_all):
        scores = (
            jnp.einsum("sqhe,skhe->shkq", queries, key_all, preferred_element_type=jnp.float32)
            * score_scale
        )
        return jnp.where(visible, scores, -1e30)

    hidden = tokens.astype(jnp.float32).reshape(rows_here, model_width)
    stored = []
    for layer_index in range(LAYERS):
        qkv_all = multiply(hidden.astype(jnp.bfloat16), w_qkv[layer_index]) + b_qkv[layer_index]
        qkv_low = qkv_all.astype(jnp.bfloat16).reshape(seqs_here, tok_here, 3 * model_width)
        queries = split_heads(qkv_low[:, :, :model_width])
        window = extended(qkv_low[:, :, model_width:], (("wide", 1),), rim_rows)
        key_all = with_prefix(layer_index, 0, window[:, :, :model_width])
        value_all = with_prefix(layer_index, 1, window[:, :, model_width:])
        scores = score_block(queries, key_all)
        top_score = jnp.max(scores, axis=2, keepdims=True)
        exp_scores = jnp.exp(scores - top_score)
        denominator = jnp.sum(exp_scores, axis=2, keepdims=True)
        probs_low = (exp_scores / denominator).astype(jnp.bfloat16)
        log_total = top_score + jnp.log(denominator)
        context = jnp.einsum(
            "shkq,skhe->sqhe", probs_low, value_all, preferred_element_type=jnp.float32
        )
        context_low = context.astype(jnp.bfloat16).reshape(rows_here, model_width)
        attention = multiply(context_low, w_out[layer_index]) + b_out[layer_index]
        pre_norm = hidden + attention
        normed = normalize(pre_norm, norm_gain[layer_index, 0], norm_bias[layer_index, 0])
        normed_low = normed.astype(jnp.bfloat16)
        up_rows = lax.all_gather(w_up[layer_index], "wide", axis=0, tiled=True)
        down_rows = lax.all_gather(w_down[layer_index], "wide", axis=0, tiled=True)
        bias_rows = lax.all_gather(b_up[layer_index], "wide", axis=0, tiled=True)
        pre_rows = multiply_back(normed_low, up_rows) + bias_rows.astype(jnp.float32)
        ffn_out = multiply(gelu_exact(pre_rows).astype(jnp.bfloat16), down_rows)
        kept_ffn = ()
        second_in = normed + ffn_out + b_down[layer_index]
        stored.append(
            (queries, key_all, value_all, log_total, pre_norm, normed_low, second_in, kept_ffn)
        )
        hidden = normalize(second_in, norm_gain[layer_index, 1], norm_bias[layer_index, 1])
    output = hidden.astype(jnp.bfloat16).reshape(seqs_here, tok_here, model_width)
    grad_hidden = cotangent.astype(jnp.float32).reshape(rows_here, model_width)
    prefix_grads = [None] * LAYERS
    for layer_index in reversed(range(LAYERS)):
        queries, key_all, value_all, log_total, pre_norm, normed_low, second_in, kept_ffn = stored[
            layer_index
        ]
        grad_sum2 = norm_grad(
            second_in, norm_gain[layer_index, 1], norm_bias[layer_index, 1], grad_hidden
        )
        grad_ffn_low = grad_sum2.astype(jnp.bfloat16)
        back_up_rows = lax.all_gather(w_up[layer_index], "wide", axis=0, tiled=True)
        back_down_rows = lax.all_gather(w_down[layer_index], "wide", axis=0, tiled=True)
        back_bias_rows = lax.all_gather(b_up[layer_index], "wide", axis=0, tiled=True)
        back_pre_rows = multiply_back(normed_low, back_up_rows) + back_bias_rows.astype(jnp.float32)
        grad_rows = gelu_back(back_pre_rows, multiply_back(grad_ffn_low, back_down_rows)).astype(
            jnp.bfloat16
        )
        grad_from_ffn = multiply(grad_rows, back_up_rows)
        grad_normed = grad_sum2 + grad_from_ffn
        grad_sum1 = norm_grad(
            pre_norm, norm_gain[layer_index, 0], norm_bias[layer_index, 0], grad_normed
        )
        grad_attn_low = grad_sum1.astype(jnp.bfloat16)
        grad_context = multiply_back(grad_attn_low, w_out[layer_index]).astype(jnp.bfloat16)
        grad_context = split_heads(grad_context.reshape(seqs_here, tok_here, model_width))
        scores = score_block(queries, key_all)
        probs = jnp.exp(scores - log_total)
        probs_low = probs.astype(jnp.bfloat16)
        grad_probs = jnp.einsum(
            "sqhe,skhe->shkq", grad_context, value_all, preferred_element_type=jnp.float32
        )
        row_dot = jnp.sum(probs * grad_probs, axis=2, keepdims=True)
        grad_scores = (probs * (grad_probs - row_dot)).astype(jnp.bfloat16)
        grad_queries = (
            jnp.einsum("shkq,skhe->sqhe", grad_scores, key_all, preferred_element_type=jnp.float32)
            * score_scale
        )
        grad_keys = (
            jnp.einsum("shkq,sqhe->skhe", grad_scores, queries, preferred_element_type=jnp.float32)
            * score_scale
        )
        grad_values = jnp.einsum(
            "shkq,sqhe->skhe", probs_low, grad_context, preferred_element_type=jnp.float32
        )
        key_count = grad_keys.shape[1]
        grad_keys = grad_keys.reshape(seqs_here, key_count, model_width)
        grad_values = grad_values.reshape(seqs_here, key_count, model_width)
        prefix_grads[layer_index] = jnp.stack(
            [
                jnp.sum(grad_keys[:, :prefix_len], axis=0),
                jnp.sum(grad_values[:, :prefix_len], axis=0),
            ],
            axis=0,
        )
        grad_window = jnp.concatenate(
            [grad_keys[:, prefix_len:], grad_values[:, prefix_len:]], axis=2
        )
        grad_kv = grad_window[:, rim_rows : rim_rows + tok_here]
        rim_grads = jnp.concatenate(
            [grad_window[:, :rim_rows], grad_window[:, rim_rows + tok_here :]], axis=1
        )
        returned = extended(rim_grads.astype(jnp.bfloat16), (("wide", 1),), rim_rows).astype(
            rim_grads.dtype
        )
        grad_kv = grad_kv + returned[:, :rim_rows]
        grad_kv = grad_kv + returned[:, 3 * rim_rows :]
        grad_qkv = jnp.concatenate(
            [grad_queries.reshape(seqs_here, tok_here, model_width), grad_kv], axis=2
        )
        grad_qkv = grad_qkv.astype(jnp.bfloat16).reshape(rows_here, 3 * model_width)
        grad_hidden = grad_sum1 + multiply_back(grad_qkv, w_qkv[layer_index])
    grad_prefix = lax.psum(jnp.stack(prefix_grads, axis=0), ("rows", "wide"))
    return (output, grad_hidden.reshape(seqs_here, tok_here, model_width), grad_prefix)


def solution(mesh):
    return jax.shard_map(
        local,
        mesh=mesh,
        in_specs=(
            P("rows", "wide", None),
            P("rows", None),
            P(),
            P(),
            P(),
            P(),
            P(),
            P(),
            P(None, "wide", None),
            P(None, "wide"),
            P(None, "wide", None),
            P(),
            P(),
            P("rows", "wide", None),
        ),
        out_specs=(P("rows", "wide", None), P("rows", "wide", None), P()),
        check_vma=False,
    )
```

profile of v0, /device:TPU:0, one launch (start us, length us, event | category | flops | bytes accessed | tf_op | source)
XLA Modules:
  0.0 841.0 jit_solution(1946470250862313874)
XLA Ops:
  7.2 3.2 fusion.185
  12.1 6.5 add_convert_fusion.3
  21.5 4.4 collective-permute-start
  25.9 2.3 slice.241
  28.2 91.8 %all-gather.1 = bf16[1,4096]{1,0:T(2,128)(2,1)S(1)} all-gather(bf16[1,512]{1,0:T(2,128)(2,1)S(1)} %get-tuple-element.50), channel_id=3, replica_groups=mesh['rows'=4,'wide'=8] {'wide'}, dimensions={1}, use_global_device_ids=true | all-gather | bytes 9216 | tf_op jit(solution)/shard_map/all_gather | solution.py:126
  126.4 3.4 pad_maximum_fusion.2
  130.9 3.4 pad_maximum_fusion.4
  134.3 6.1 copy.49
  140.4 6.7 copy.50
  147.1 10.5 %fusion.193 = (f32[4,16,128]{2,1,0:T(8,128)S(1)}, f32[4,16,448,128]{3,2,1,0:T(8,128)}) fusion(bf16[4,448,16,64]{1,3,2,0:T(8,128)(2,1)} %bitcast.215, bf16[4,128,16,64]{1,3,2,0:T(8,128)(2,1)S(1)} %bitcast.223, pred[4,448,128]{2,1,0:T(8,128)(4,1)S(1)} %concatenate.59), kind=kOutput, calls=%fused_computation.264 | convolution fusion | flops 480763904 | bytes 19660800 | tf_op jit(solution)/shard_map/sqhe,skhe->shkq/dot_general | solution.py:96
  157.6 9.0 %fusion = f32[4,16,128]{2,1,0:T(8,128)S(1)} fusion(f32[4,16,448,128]{3,2,1,0:T(8,128)} %get-tuple-element.52, f32[4,16,128]{2,1,0:T(8,128)S(1)} %get-tuple-element.51), kind=kLoop, calls=%fused_computation.18 | loop fusion | flops 7331840 | bytes 14745600 | tf_op jit(solution)/shard_map/reduce_sum | solution.py:113
  166.7 8.5 %fusion.134 = bf16[4,128,16,64]{1,3,2,0:T(8,128)(2,1)S(1)} fusion(bf16[4,448,16,64]{1,3,2,0:T(8,128)(2,1)S(1)} %bitcast.227, f32[4,16,448,128]{3,2,1,0:T(8,128)} %get-tuple-element.52, f32[4,16,128]{2,1,0:T(8,128)S(1)} %fusion, f32[4,16,128]{2,1,0:T(8,128)S(1)} %get-tuple-element.51), kind=kOutput, calls=%fused_computation.183 | convolution fusion | flops 481296384 | bytes 19464192 | tf_op jit(solution)/shard_map/shkq,skhe->sqhe/dot_general | solution.py:116
  178.0 27.0 %fusion.6 = (f32[512,4096]{1,0:T(8,128)}, f32[512,4096]{1,0:T(8,128)}) fusion(f32[4096]{0:T(1024)S(1)} %bitcast.247, bf16[1,4096,1024]{2,1,0:T(8,128)(2,1)} %all-gather.11.cloned.1.call-done, f32[512,1024]{1,0:T(8,128)S(1)} %get-tuple-element.54, f32[1024]{0:T(1024)} %bitcast.272, f32[1024]{0:T(1024)S(1)} %bitcast.259, f32[512]{0:T(512)S(1)} %fusion.163, ...), kind=kOutput, calls=%fused_computation.26 | convolution fusion | flops 4429709312 | bytes 27291648 | tf_op jit(solution)/shard_map/dot_general | solution.py:48
  205.0 12.3 %fusion.195 = (f32[512]{0:T(512)S(1)}, f32[512,1024]{1,0:T(8,128)S(1)}) fusion(f32[1024]{0:T(1024)S(1)} %bitcast.257, bf16[1,4096,1024]{2,1,0:T(8,128)(2,1)} %all-gather.13.cloned.1.call-done, f32[512,4096]{1,0:T(8,128)} %get-tuple-element.55, f32[512,4096]{1,0:T(8,128)} %get-tuple-element.56, f32[4096]{0:T(1024)S(1)} %bitcast.248, ...), kind=kOutput, calls=%fused_computation.266 | convolution fusion | flops 4307025408 | bytes 29394944 | tf_op jit(solution)/shard_map/dot_general | solution.py:44
  217.7 7.1 add_convert_fusion.2
  227.7 4.4 collective-permute-start.2
  232.2 74.9 %all-gather.4 = bf16[1,4096]{1,0:T(2,128)(2,1)S(1)} all-gather(bf16[1,512]{1,0:T(2,128)(2,1)S(1)} %get-tuple-element.49), channel_id=6, replica_groups=mesh['rows'=4,'wide'=8] {'wide'}, dimensions={1}, use_global_device_ids=true | all-gather | bytes 9216 | tf_op jit(solution)/shard_map/all_gather | solution.py:126
  311.0 3.8 pad_maximum_fusion.3
  314.8 2.5 fusion.183
  319.5 6.1 copy.54
  325.7 4.1 pad_maximum_fusion.6
  329.9 6.3 copy.53
  336.2 10.6 %fusion.196 = (f32[4,16,128]{2,1,0:T(8,128)S(1)}, f32[4,16,448,128]{3,2,1,0:T(8,128)}) fusion(bf16[4,448,16,64]{1,3,2,0:T(8,128)(2,1)} %bitcast.217, bf16[4,128,16,64]{1,3,2,0:T(8,128)(2,1)S(1)} %bitcast.225, pred[4,448,128]{2,1,0:T(8,128)(4,1)S(1)} %concatenate.59), kind=kOutput, calls=%fused_computation.267 | convolution fusion | flops 480763904 | bytes 19660800 | tf_op jit(solution)/shard_map/sqhe,skhe->shkq/dot_general | solution.py:96
  346.8 9.1 %fusion.1 = f32[4,16,128]{2,1,0:T(8,128)S(1)} fusion(f32[4,16,448,128]{3,2,1,0:T(8,128)} %get-tuple-element.60, f32[4,16,128]{2,1,0:T(8,128)S(1)} %get-tuple-element.59), kind=kLoop, calls=%fused_computation.19 | loop fusion | flops 7331840 | bytes 14745600 | tf_op jit(solution)/shard_map/reduce_sum | solution.py:113
  355.9 8.6 %fusion.135 = bf16[4,128,16,64]{1,3,2,0:T(8,128)(2,1)S(1)} fusion(bf16[4,448,16,64]{1,3,2,0:T(8,128)(2,1)S(1)} %bitcast.229, f32[4,16,448,128]{3,2,1,0:T(8,128)} %get-tuple-element.60, f32[4,16,128]{2,1,0:T(8,128)S(1)} %fusion.1, f32[4,16,128]{2,1,0:T(8,128)S(1)} %get-tuple-element.59), kind=kOutput, calls=%fused_computation.184 | convolution fusion | flops 481296384 | bytes 19464192 | tf_op jit(solution)/shard_map/shkq,skhe->sqhe/dot_general | solution.py:116
  367.9 26.7 %fusion.7 = (f32[512,4096]{1,0:T(8,128)}, f32[512,4096]{1,0:T(8,128)}) fusion(f32[4096]{0:T(1024)S(1)} %bitcast.250, bf16[1,4096,1024]{2,1,0:T(8,128)(2,1)} %all-gather.15.cloned.1.call-done, f32[512,1024]{1,0:T(8,128)S(1)} %get-tuple-element.62, f32[1024]{0:T(1024)S(1)} %bitcast.268, f32[1024]{0:T(1024)S(1)} %bitcast.265, f32[512]{0:T(512)S(1)} %fusion.165, ...), kind=kOutput, calls=%fused_computation.27 | convolution fusion | flops 4429709312 | bytes 27291648 | tf_op jit(solution)/shard_map/dot_general | solution.py:48
  394.6 11.0 %fusion.198 = (f32[512]{0:T(512)S(1)}, f32[512,1024]{1,0:T(8,128)S(1)}) fusion(f32[1024]{0:T(1024)S(1)} %bitcast.255, bf16[1,4096,1024]{2,1,0:T(8,128)(2,1)} %all-gather.17.cloned.1.call-done, f32[512,4096]{1,0:T(8,128)} %get-tuple-element.63, f32[512,4096]{1,0:T(8,128)} %get-tuple-element.64, f32[4096]{0:T(1024)S(1)} %bitcast.251, ...), kind=kOutput, calls=%fused_computation.269 | convolution fusion | flops 4307025408 | bytes 29394944 | tf_op jit(solution)/shard_map/dot_general | solution.py:44
  406.2 2.6 fusion.180
  408.8 23.4 %multiply_reduce_fusion.4 = (f32[512]{0:T(512)S(1)}, f32[512,1024]{1,0:T(8,128)}) fusion(f32[512,1024]{1,0:T(8,128)S(1)} %get-tuple-element.62, f32[512]{0:T(512)S(1)} %broadcast_multiply_fusion.3, f32[1024]{0:T(1024)S(1)} %bitcast.267, bf16[1,4096,1024]{2,1,0:T(8,128)(2,1)} %all-gather.15.cloned.1.call-done, f32[512,4096]{1,0:T(8,128)} %get-tuple-element.63, ...), kind=kOutput, calls=%fused_computation.153 | convolution fusion | flops 8625586176 | bytes 39872512 | tf_op jit(solution)/shard_map/dot_general | solution.py:44
  432.3 2.3 fusion.179
  440.4 12.0 %fusion.36 = f32[4,16,64,448]{3,2,1,0:T(8,128)} fusion(bf16[4,128,16,64]{1,3,2,0:T(8,128)(2,1)S(1)} %copy.58, f32[4,16,448,128]{3,2,1,0:T(8,128)} %get-tuple-element.60, f32[4,16,128]{2,1,0:T(8,128)S(1)} %log_add_fusion.1), kind=kOutput, calls=%fused_computation.75 | convolution fusion | flops 477102080 | bytes 23101440 | tf_op jit(solution)/shard_map/shkq,sqhe->skhe/dot_general | solution.py:177
  452.4 10.4 %multiply_reduce_fusion.1 = (f32[4,16,128]{2,1,0:T(8,128)S(1)}, f32[4,16,448,128]{3,2,1,0:T(8,128)}) fusion(f32[4,16,448,128]{3,2,1,0:T(8,128)} %get-tuple-element.60, f32[4,16,128]{2,1,0:T(8,128)S(1)} %log_add_fusion.1, bf16[4,448,16,64]{1,3,2,0:T(8,128)(2,1)S(1)} %bitcast.230, bf16[4,128,16,64]{1,3,2,0:T(8,128)(2,1)S(1)} %copy.58), kind=kOutput, calls=%fused_computation.10 | convolution fusion | flops 480763904 | bytes 34144256 | tf_op jit(solution)/shard_map/sqhe,skhe->shkq/dot_general | solution.py:164
  462.8 7.9 slice.247
  470.6 6.6 copy.81
  477.2 10.5 %multiply_convert_fusion.1 = bf16[4,16,448,128]{3,2,1,0:T(8,128)(2,1)S(1)} fusion(f32[4,16,448,128]{3,2,1,0:T(8,128)} %get-tuple-element.70, f32[4,16,448,128]{3,2,1,0:T(8,128)} %get-tuple-element.60, f32[4,16,128]{2,1,0:T(8,128)S(1)} %get-tuple-element.69, f32[4,16,128]{2,1,0:T(8,128)S(1)} %log_add_fusion.1), kind=kLoop, calls=%fused_computation.9 | loop fusion | flops 14680064 | bytes 36765696 | tf_op jit(solution)/shard_map/convert_element_type | solution.py:168
  487.7 3.2 broadcast_multiply_fusion.1
  491.0 3.3 copy-done.2
  494.3 4.3 slice.246
  498.6 6.6 copy.80
  505.2 8.2 fusion.3
  513.4 4.9 fusion.182
  518.4 3.5 collective-permute-start.4
  523.2 4.8 fusion.136
  531.6 4.1 fusion.61
  536.3 6.6 multiply_reduce_fusion.3
  544.9 23.6 %multiply_reduce_fusion.2 = (f32[512]{0:T(512)S(1)}, f32[512,1024]{1,0:T(8,128)}) fusion(f32[512,1024]{1,0:T(8,128)S(1)} %copy-done.14, f32[512]{0:T(512)S(1)} %copy-done.35, f32[1024]{0:T(1024)S(1)} %bitcast.261, bf16[1,4096,1024]{2,1,0:T(8,128)(2,1)} %all-gather.11.cloned.1.call-done, f32[512,4096]{1,0:T(8,128)} %get-tuple-element.55, ...), kind=kOutput, calls=%fused_computation.148 | convolution fusion | flops 8625586176 | bytes 39872512 | tf_op jit(solution)/shard_map/dot_general | solution.py:44
  568.5 2.3 fusion.177
  576.6 11.8 %fusion.34 = f32[4,16,64,448]{3,2,1,0:T(8,128)} fusion(bf16[4,128,16,64]{1,3,2,0:T(8,128)(2,1)S(1)} %copy.65, f32[4,16,448,128]{3,2,1,0:T(8,128)} %get-tuple-element.52, f32[4,16,128]{2,1,0:T(8,128)S(1)} %log_add_fusion), kind=kOutput, calls=%fused_computation.74 | convolution fusion | flops 477102080 | bytes 23101440 | tf_op jit(solution)/shard_map/shkq,sqhe->skhe/dot_general | solution.py:177
  588.5 10.1 %multiply_reduce_fusion = (f32[4,16,128]{2,1,0:T(8,128)S(1)}, f32[4,16,448,128]{3,2,1,0:T(8,128)}) fusion(f32[4,16,448,128]{3,2,1,0:T(8,128)} %get-tuple-element.52, f32[4,16,128]{2,1,0:T(8,128)S(1)} %log_add_fusion, bf16[4,448,16,64]{1,3,2,0:T(8,128)(2,1)S(1)} %bitcast.228, bf16[4,128,16,64]{1,3,2,0:T(8,128)(2,1)S(1)} %copy.65), kind=kOutput, calls=%fused_computation.7 | convolution fusion | flops 480763904 | bytes 34144256 | tf_op jit(solution)/shard_map/sqhe,skhe->shkq/dot_general | solution.py:164
  598.6 7.7 slice.253
  606.3 6.6 copy.83
  612.9 10.7 %multiply_convert_fusion = bf16[4,16,448,128]{3,2,1,0:T(8,128)(2,1)S(1)} fusion(f32[4,16,448,128]{3,2,1,0:T(8,128)} %get-tuple-element.76, f32[4,16,448,128]{3,2,1,0:T(8,128)} %get-tuple-element.52, f32[4,16,128]{2,1,0:T(8,128)S(1)} %get-tuple-element.75, f32[4,16,128]{2,1,0:T(8,128)S(1)} %log_add_fusion), kind=kLoop, calls=%fused_computation.6 | loop fusion | flops 14680064 | bytes 36765696 | tf_op jit(solution)/shard_map/convert_element_type | solution.py:168
  623.6 3.2 broadcast_multiply_fusion
  626.9 3.3 copy-done.3
  630.1 4.3 slice.252
  634.4 6.6 copy.82
  641.0 8.2 fusion.2
  649.3 4.9 fusion.181
  654.1 19.9 %collective-permute-start.6 = (bf16[4,128,2048]{2,1,0:T(8,128)(2,1)}, bf16[4,128,2048]{2,1,0:T(8,128)(2,1)}, u32[]{:S(2)}, u32[]{:S(2)}) collective-permute-start(bf16[4,128,2048]{2,1,0:T(8,128)(2,1)} %get-tuple-element.16), channel_id=1, source_target_pairs={{0,1},{1,2},{2,3},{3,4},{4,5},{5,6},{6,7},{8,9},{9,10},{10,11},{11... | collective-permute-start | bytes 6291464 | tf_op jit(solution)/shard_map/ppermute | solution.py:17
  684.1 6.0 fusion.137
  693.5 125.9 %all-reduce.4.cloned.1.call-done = f32[2,2,64,1024]{2,3,1,0:T(8,128)} async-done(((f32[2,2,64,1024]{2,3,1,0:T(8,128)}), f32[2,2,64,1024]{2,3,1,0:T(8,128)}) %all-reduce.4.cloned.1.call-update) | async-done | bytes 1048592 | tf_op jit(solution)/shard_map/psum | solution.py:207
  819.4 3.1 copy.71
  822.6 4.0 fusion.57
  826.6 7.5 add_add_fusion.8
  (232 shorter events, 60.6 us)
Async XLA Ops:
  7.2 4.9 copy-start.32
  7.2 4.9 copy-start.68
  7.2 170.8 %all-gather.11.cloned.1.call-start = ((), (), s32[]{:S(2)}) async-start(), calls=%async_computation.1 | async-start | bytes 9437184 | tf_op jit(solution)/shard_map/all_gather | solution.py:124
  10.4 194.5 %all-gather.13.cloned.1.call-start = ((), (), s32[]{:S(2)}) async-start(), calls=%async_computation.2 | async-start | bytes 9437184 | tf_op jit(solution)/shard_map/all_gather | solution.py:125
  12.0 355.8 %all-gather.15.cloned.1.call-start = ((), (), s32[]{:S(2)}) async-start(), calls=%async_computation.3 | async-start | bytes 9437184 | tf_op jit(solution)/shard_map/all_gather | solution.py:124
  18.6 9.6 %copy-start.53 = (bf16[2,512]{1,0:T(2,128)(2,1)S(1)}, bf16[2,512]{1,0:T(2,128)(2,1)}, u32[]{:S(2)}) copy-start(bf16[2,512]{1,0:T(2,128)(2,1)} %param.23) | copy-start | bytes 6148
  18.6 103.1 %copy-start.33 = (s32[4,1024]{1,0:T(4,128)S(1)}, s32[4,1024]{1,0:T(4,128)}, u32[]{:S(2)}) copy-start(s32[4,1024]{1,0:T(4,128)} %param.15) | copy-start | bytes 49156
  18.6 103.4 %copy-start.51 = (f32[2,1024]{1,0:T(2,128)S(1)}, f32[2,1024]{1,0:T(2,128)}, u32[]{:S(2)}) copy-start(f32[2,1024]{1,0:T(2,128)} %param.19) | copy-start | bytes 24580
  18.6 104.0 %copy-start.52 = (f32[2,1024]{1,0:T(2,128)S(1)}, f32[2,1024]{1,0:T(2,128)}, u32[]{:S(2)}) copy-start(f32[2,1024]{1,0:T(2,128)} %param.25) | copy-start | bytes 24580
  18.6 104.6 %copy-start.43 = (f32[2,2,1024]{2,1,0:T(2,128)S(1)}, f32[2,2,1024]{2,1,0:T(2,128)}, u32[]{:S(2)}) copy-start(f32[2,2,1024]{2,1,0:T(2,128)} %param.20) | copy-start | bytes 49156
  18.6 105.2 %copy-start.44 = (f32[2,2,1024]{2,1,0:T(2,128)S(1)}, f32[2,2,1024]{2,1,0:T(2,128)}, u32[]{:S(2)}) copy-start(f32[2,2,1024]{2,1,0:T(2,128)} %param.21) | copy-start | bytes 49156
  20.2 106.2 %collective-permute-start.1 = (bf16[4,128,2048]{2,1,0:T(8,128)(2,1)S(1)}, bf16[4,128,2048]{2,1,0:T(8,128)(2,1)}, u32[]{:S(2)}, u32[]{:S(2)}) collective-permute-start(bf16[4,128,2048]{2,1,0:T(8,128)(2,1)S(1)} %slice.238), channel_id=1, source_target_pairs={{1,0},{2,1},{3,2},{4,3},{5,4},{6,5},{7,6},{9,8},{10,9},{11,10},{12... | collective-permute-start | bytes 6291464 | tf_op jit(solution)/shard_map/ppermute | solution.py:20
  21.5 104.9 %collective-permute-start = (bf16[4,128,2048]{2,1,0:T(8,128)(2,1)S(1)}, bf16[4,128,2048]{2,1,0:T(8,128)(2,1)}, u32[]{:S(2)}, u32[]{:S(2)}) collective-permute-start(bf16[4,128,2048]{2,1,0:T(8,128)(2,1)S(1)} %slice.238), channel_id=1, source_target_pairs={{0,1},{1,2},{2,3},{3,4},{4,5},{5,6},{6,7},{8,9},{9,10},{10,11},{11... | collective-permute-start | bytes 6291464 | tf_op jit(solution)/shard_map/ppermute | solution.py:17
  25.9 368.6 %all-gather.17.cloned.1.call-start = ((), (), s32[]{:S(2)}) async-start(), calls=%async_computation.4 | async-start | bytes 9437184 | tf_op jit(solution)/shard_map/all_gather | solution.py:125
  120.0 84.9 %copy-start.45 = (f32[1,4096]{1,0:T(1,128)}, f32[1,4096]{1,0:T(1,128)S(1)}, u32[]{:S(2)}) copy-start(f32[1,4096]{1,0:T(1,128)S(1)} %convert_element_type.132) | copy-start | bytes 49156
  121.7 25.4 %copy-start.5 = (bf16[4,128,1024]{1,2,0:T(8,128)(2,1)}, bf16[4,128,1024]{1,2,0:T(8,128)(2,1)S(1)}, u32[]{:S(2)}) copy-start(bf16[4,128,1024]{1,2,0:T(8,128)(2,1)S(1)} %copy.51) | copy-start | bytes 3145732
  123.8 81.1 %copy-start.56 = (f32[1,1,1024]{2,1,0:T(1,128)}, f32[1,1,1024]{2,1,0:T(1,128)S(1)}, u32[]{:S(2)}) copy-start(f32[1,1,1024]{2,1,0:T(1,128)S(1)} %get-tuple-element.37) | copy-start | bytes 12292
  123.8 241.5 %copy-start.58 = (f32[1,1,1024]{2,1,0:T(1,128)}, f32[1,1,1024]{2,1,0:T(1,128)S(1)}, u32[]{:S(2)}) copy-start(f32[1,1,1024]{2,1,0:T(1,128)S(1)} %get-tuple-element.36) | copy-start | bytes 12292
  157.6 9.1 %copy-start.27 = (f32[4,16,128]{2,1,0:T(8,128)}, f32[4,16,128]{2,1,0:T(8,128)S(1)}, u32[]{:S(2)}) copy-start(f32[4,16,128]{2,1,0:T(8,128)S(1)} %get-tuple-element.51) | copy-start | bytes 98308
  157.6 9.1 %copy-start.9 = (bf16[4,448,1024]{1,2,0:T(8,128)(2,1)S(1)}, bf16[4,448,1024]{1,2,0:T(8,128)(2,1)}, u32[]{:S(2)}) copy-start(bf16[4,448,1024]{1,2,0:T(8,128)(2,1)} %copy.49) | copy-start | bytes 11010052
  166.6 8.6 %copy-start.29 = (f32[4,16,128]{2,1,0:T(8,128)}, f32[4,16,128]{2,1,0:T(8,128)S(1)}, u32[]{:S(2)}) copy-start(f32[4,16,128]{2,1,0:T(8,128)S(1)} %fusion) | copy-start | bytes 98308
  166.7 9.4 %copy-start.64 = (bf16[2,1024,1024]{2,1,0:T(8,128)(2,1)S(1)}, bf16[2,1024,1024]{2,1,0:T(8,128)(2,1)}, u32[]{:S(2)}) copy-start(bf16[2,1024,1024]{2,1,0:T(8,128)(2,1)} %param.18) | copy-start | bytes 12582916
  166.7 9.4 %copy-start.69 = (bf16[4,128,1024]{2,1,0:T(8,128)(2,1)S(1)}, bf16[4,128,1024]{2,1,0:T(8,128)(2,1)}, u32[]{:S(2)}) copy-start(bf16[4,128,1024]{2,1,0:T(8,128)(2,1)} %param.14) | copy-start | bytes 3145732
  177.5 27.4 %copy-start.13 = (f32[512,1024]{1,0:T(8,128)}, f32[512,1024]{1,0:T(8,128)S(1)}, u32[]{:S(2)}) copy-start(f32[512,1024]{1,0:T(8,128)S(1)} %get-tuple-element.54) | copy-start | bytes 6291460
  177.6 27.4 %copy-start.34 = (f32[512]{0:T(512)}, f32[512]{0:T(512)S(1)}, u32[]{:S(2)}) copy-start(f32[512]{0:T(512)S(1)} %broadcast_multiply_fusion.5) | copy-start | bytes 6148
  177.9 27.0 %copy-start.38 = (f32[512]{0:T(512)}, f32[512]{0:T(512)S(1)}, u32[]{:S(2)}) copy-start(f32[512]{0:T(512)S(1)} %multiply_reduce_fusion.8) | copy-start | bytes 6148
  177.9 27.1 %copy-start.47 = (f32[512]{0:T(512)}, f32[512]{0:T(512)S(1)}, u32[]{:S(2)}) copy-start(f32[512]{0:T(512)S(1)} %fusion.163) | copy-start | bytes 6148
  178.0 27.0 %copy-start.63 = (f32[1,1,1024]{2,1,0:T(1,128)S(1)}, f32[1,1,1024]{2,1,0:T(1,128)}, u32[]{:S(2)}) copy-start(f32[1,1,1024]{2,1,0:T(1,128)} %get-tuple-element.41) | copy-start | bytes 12292
  205.0 12.7 %copy-start.62 = (f32[1,1,1024]{2,1,0:T(1,128)S(1)}, f32[1,1,1024]{2,1,0:T(1,128)}, u32[]{:S(2)}) copy-start(f32[1,1,1024]{2,1,0:T(1,128)} %get-tuple-element.40) | copy-start | bytes 12292
  217.3 7.5 copy-start.15
  217.3 148.0 %copy-start.36 = (f32[512]{0:T(512)}, f32[512]{0:T(512)S(1)}, u32[]{:S(2)}) copy-start(f32[512]{0:T(512)S(1)} %broadcast_multiply_fusion.4) | copy-start | bytes 6148
  217.7 7.1 copy-start.40
  217.7 147.6 %copy-start.49 = (f32[512]{0:T(512)}, f32[512]{0:T(512)S(1)}, u32[]{:S(2)}) copy-start(f32[512]{0:T(512)S(1)} %fusion.164) | copy-start | bytes 6148
  226.4 84.6 %collective-permute-start.3 = (bf16[4,128,2048]{2,1,0:T(8,128)(2,1)S(1)}, bf16[4,128,2048]{2,1,0:T(8,128)(2,1)}, u32[]{:S(2)}, u32[]{:S(2)}) collective-permute-start(bf16[4,128,2048]{2,1,0:T(8,128)(2,1)S(1)} %slice.242), channel_id=1, source_target_pairs={{1,0},{2,1},{3,2},{4,3},{5,4},{6,5},{7,6},{9,8},{10,9},{11,10},{12... | collective-permute-start | bytes 6291464 | tf_op jit(solution)/shard_map/ppermute | solution.py:20
  227.7 83.3 %collective-permute-start.2 = (bf16[4,128,2048]{2,1,0:T(8,128)(2,1)S(1)}, bf16[4,128,2048]{2,1,0:T(8,128)(2,1)}, u32[]{:S(2)}, u32[]{:S(2)}) collective-permute-start(bf16[4,128,2048]{2,1,0:T(8,128)(2,1)S(1)} %slice.242), channel_id=1, source_target_pairs={{0,1},{1,2},{2,3},{3,4},{4,5},{5,6},{6,7},{8,9},{9,10},{10,11},{11... | collective-permute-start | bytes 6291464 | tf_op jit(solution)/shard_map/ppermute | solution.py:17
  232.1 587.3 %all-reduce.4.cloned.1.call-start = ((), (), s32[]{:S(2)}) async-start(), calls=%async_computation | async-start | bytes 4194304 | tf_op jit(solution)/shard_map/psum | solution.py:207
  311.0 25.2 %copy-start.7 = (bf16[4,128,1024]{1,2,0:T(8,128)(2,1)}, bf16[4,128,1024]{1,2,0:T(8,128)(2,1)S(1)}, u32[]{:S(2)}) copy-start(bf16[4,128,1024]{1,2,0:T(8,128)(2,1)S(1)} %copy.55) | copy-start | bytes 3145732
  346.8 9.1 %copy-start.11 = (bf16[4,448,1024]{1,2,0:T(8,128)(2,1)S(1)}, bf16[4,448,1024]{1,2,0:T(8,128)(2,1)}, u32[]{:S(2)}) copy-start(bf16[4,448,1024]{1,2,0:T(8,128)(2,1)} %copy.53) | copy-start | bytes 11010052
  355.8 9.5 %copy-start.16 = (f32[512,1024]{1,0:T(8,128)S(1)}, f32[512,1024]{1,0:T(8,128)}, u32[]{:S(2)}) copy-start(f32[512,1024]{1,0:T(8,128)} %copy-done.15) | copy-start | bytes 6291460
  355.8 9.5 %copy-start.55 = (f32[1,1024]{1,0:T(1,128)S(1)}, f32[1,1024]{1,0:T(1,128)}, u32[]{:S(2)}) copy-start(f32[1,1024]{1,0:T(1,128)} %get-tuple-element.45) | copy-start | bytes 12292
  355.8 9.5 %copy-start.65 = (bf16[2,1024,1024]{2,1,0:T(8,128)(2,1)S(1)}, bf16[2,1024,1024]{2,1,0:T(8,128)(2,1)}, u32[]{:S(2)}) copy-start(bf16[2,1024,1024]{2,1,0:T(8,128)(2,1)} %param.18) | copy-start | bytes 12582916
  367.9 26.7 %copy-start.54 = (f32[1,1024]{1,0:T(1,128)S(1)}, f32[1,1024]{1,0:T(1,128)}, u32[]{:S(2)}) copy-start(f32[1,1024]{1,0:T(1,128)} %get-tuple-element.43) | copy-start | bytes 12292
  394.5 11.0 %copy-start.18 = (bf16[4,128,1024]{2,1,0:T(8,128)(2,1)S(1)}, bf16[4,128,1024]{2,1,0:T(8,128)(2,1)}, u32[]{:S(2)}) copy-start(bf16[4,128,1024]{2,1,0:T(8,128)(2,1)} %param.27) | copy-start | bytes 3145732
  394.5 11.0 %copy-start.31 = (f32[1,1,1024]{2,1,0:T(1,128)S(1)}, f32[1,1,1024]{2,1,0:T(1,128)}, u32[]{:S(2)}) copy-start(f32[1,1,1024]{2,1,0:T(1,128)} %get-tuple-element.35) | copy-start | bytes 12292
  394.5 11.7 %copy-start.42 = (f32[1,1,1024]{2,1,0:T(1,128)S(1)}, f32[1,1,1024]{2,1,0:T(1,128)}, u32[]{:S(2)}) copy-start(f32[1,1,1024]{2,1,0:T(1,128)} %get-tuple-element.39) | copy-start | bytes 12292
  440.4 12.0 %copy-start.12 = (bf16[4,448,1024]{1,2,0:T(8,128)(2,1)S(1)}, bf16[4,448,1024]{1,2,0:T(8,128)(2,1)}, u32[]{:S(2)}) copy-start(bf16[4,448,1024]{1,2,0:T(8,128)(2,1)} %copy.53) | copy-start | bytes 11010052
  477.2 10.5 %copy-start.8 = (bf16[4,128,1024]{1,2,0:T(8,128)(2,1)S(1)}, bf16[4,128,1024]{1,2,0:T(8,128)(2,1)}, u32[]{:S(2)}) copy-start(bf16[4,128,1024]{1,2,0:T(8,128)(2,1)} %copy-done.7) | copy-start | bytes 3145732
  513.4 9.7 %copy-start.28 = (f32[4,16,128]{2,1,0:T(8,128)S(1)}, f32[4,16,128]{2,1,0:T(8,128)}, u32[]{:S(2)}) copy-start(f32[4,16,128]{2,1,0:T(8,128)} %copy-done.27) | copy-start | bytes 98308
  513.4 9.7 %copy-start.30 = (f32[4,16,128]{2,1,0:T(8,128)S(1)}, f32[4,16,128]{2,1,0:T(8,128)}, u32[]{:S(2)}) copy-start(f32[4,16,128]{2,1,0:T(8,128)} %copy-done.29) | copy-start | bytes 98308
  513.4 9.7 %copy-start.4 = (bf16[4,448,1024]{1,2,0:T(8,128)(2,1)S(1)}, bf16[4,448,1024]{1,2,0:T(8,128)(2,1)}, u32[]{:S(2)}) copy-start(bf16[4,448,1024]{1,2,0:T(8,128)(2,1)} %copy.54) | copy-start | bytes 11010052
  518.4 13.3 %collective-permute-start.4 = (bf16[4,128,2048]{2,1,0:T(8,128)(2,1)}, bf16[4,128,2048]{2,1,0:T(8,128)(2,1)}, u32[]{:S(2)}, u32[]{:S(2)}) collective-permute-start(bf16[4,128,2048]{2,1,0:T(8,128)(2,1)} %get-tuple-element.18), channel_id=1, source_target_pairs={{0,1},{1,2},{2,3},{3,4},{4,5},{5,6},{6,7},{8,9},{9,10},{10,11},{11... | collective-permute-start | bytes 6291464 | tf_op jit(solution)/shard_map/ppermute | solution.py:17
  521.8 9.8 %collective-permute-start.5 = (bf16[4,128,2048]{2,1,0:T(8,128)(2,1)}, bf16[4,128,2048]{2,1,0:T(8,128)(2,1)}, u32[]{:S(2)}, u32[]{:S(2)}) collective-permute-start(bf16[4,128,2048]{2,1,0:T(8,128)(2,1)} %get-tuple-element.19), channel_id=1, source_target_pairs={{1,0},{2,1},{3,2},{4,3},{5,4},{6,5},{7,6},{9,8},{10,9},{11,10},{12... | collective-permute-start | bytes 6291464 | tf_op jit(solution)/shard_map/ppermute | solution.py:20
  531.6 4.1 copy-start.17
  531.6 4.7 copy-start.25
  531.6 4.7 copy-start.37
  531.6 4.7 copy-start.59
  536.3 6.7 copy-start.41
  536.3 6.7 copy-start.50
  544.9 23.7 %copy-start.39 = (f32[512]{0:T(512)S(1)}, f32[512]{0:T(512)}, u32[]{:S(2)}) copy-start(f32[512]{0:T(512)} %copy-done.38) | copy-start | bytes 6148
  544.9 23.7 %copy-start.48 = (f32[512]{0:T(512)S(1)}, f32[512]{0:T(512)}, u32[]{:S(2)}) copy-start(f32[512]{0:T(512)} %copy-done.47) | copy-start | bytes 6148
  576.6 11.8 %copy-start.10 = (bf16[4,448,1024]{1,2,0:T(8,128)(2,1)S(1)}, bf16[4,448,1024]{1,2,0:T(8,128)(2,1)}, u32[]{:S(2)}) copy-start(bf16[4,448,1024]{1,2,0:T(8,128)(2,1)} %copy.49) | copy-start | bytes 11010052
  612.9 10.7 %copy-start.6 = (bf16[4,128,1024]{1,2,0:T(8,128)(2,1)S(1)}, bf16[4,128,1024]{1,2,0:T(8,128)(2,1)}, u32[]{:S(2)}) copy-start(bf16[4,128,1024]{1,2,0:T(8,128)(2,1)} %copy-done.5) | copy-start | bytes 3145732
  654.1 168.4 %collective-permute-start.6 = (bf16[4,128,2048]{2,1,0:T(8,128)(2,1)}, bf16[4,128,2048]{2,1,0:T(8,128)(2,1)}, u32[]{:S(2)}, u32[]{:S(2)}) collective-permute-start(bf16[4,128,2048]{2,1,0:T(8,128)(2,1)} %get-tuple-element.16), channel_id=1, source_target_pairs={{0,1},{1,2},{2,3},{3,4},{4,5},{5,6},{6,7},{8,9},{9,10},{10,11},{11... | collective-permute-start | bytes 6291464 | tf_op jit(solution)/shard_map/ppermute | solution.py:17
  674.0 148.6 %collective-permute-start.7 = (bf16[4,128,2048]{2,1,0:T(8,128)(2,1)}, bf16[4,128,2048]{2,1,0:T(8,128)(2,1)}, u32[]{:S(2)}, u32[]{:S(2)}) collective-permute-start(bf16[4,128,2048]{2,1,0:T(8,128)(2,1)} %get-tuple-element.17), channel_id=1, source_target_pairs={{1,0},{2,1},{3,2},{4,3},{5,4},{6,5},{7,6},{9,8},{10,9},{11,10},{12... | collective-permute-start | bytes 6291464 | tf_op jit(solution)/shard_map/ppermute | solution.py:20
  (19 other events, 48.9 us)
Sparse Core Ops, SparseCore 0:
  10.6 101.7 all-gather.10
  114.6 85.6 all-gather.12
  201.9 97.0 all-gather.14
  301.0 86.1 all-gather.16
  684.2 135.1 all-reduce.3
where the time goes:
time: 847 us; the launch traced here: 841 us
  matrix products  257 us (30%)
  blocking collectives  167 us (20%)
  local copies, waits for them, and re-layouts  137 us (16%)
  waiting for transfers between devices  126 us (15%)
  other arithmetic  101 us (12%)
  starting transfers between devices  37.4 us (4%)
  between operations  15.4 us (2%)
    all_gather x2, blocking collectives, local(): bias_rows = lax.all_gather(b_up[layer_index], 'wide', axis=0, tiled=True)  167 us
    psum x1, waiting for transfers between devices, local(): grad_prefix = lax.psum(jnp.stack(prefix_grads, axis=0), ('rows', 'wide'))  126 us
    dot_general x8, matrix products, multiply(): return jnp.dot(left, right, preferred_element_type=jnp.float32)  86.8 us
    dot_general x6, matrix products, multiply_back(): lax.dot_general(left, right, (((1,), (1,)), ((), ())), preferred_element_...  70.4 us
    unnamed x145, local copies, waits for them, and re-layouts  42.3 us
    ppermute x4, starting transfers between devices, extended(): lax.ppermute(lax.slice_in_dim(block, block.shape[dim] - width, None, axis...  32.1 us
    concatenate x4, local copies, waits for them, and re-layouts, with_prefix(): return split_heads(jnp.concatenate([fixed_rows, window_part], axis=1))  25.2 us
    another operation x4, other arithmetic  24.5 us
  transfers between devices with their start and end apart: 13, of which 1 were waited for; matrix products, arithmetic and copies ran while one was open for 28% of the time, Pallas kernels for 0%

commit v1 on v0

--- a/solution.py
+++ b/solution.py
@@ -1,3 +1,4 @@
+import functools
 import math
 import jax
 import jax.numpy as jnp
@@ -7,6 +8,13 @@
 HEADS = 16
 PAIR_MAX = 128
 LAYERS = 2
+
+
+def number_zones_for(a0, peer_axis):
+    return jax.lax.all_gather(a0, peer_axis).sum(axis=0)
+
+
+name_pipes = functools.partial(number_zones_for, peer_axis=("rows", "wide"))
 
 
 def extended(block, sides, width):
@@ -204,7 +212,7 @@
         )
         grad_qkv = grad_qkv.astype(jnp.bfloat16).reshape(rows_here, 3 * model_width)
         grad_hidden = grad_sum1 + multiply_back(grad_qkv, w_qkv[layer_index])
-    grad_prefix = lax.psum(jnp.stack(prefix_grads, axis=0), ("rows", "wide"))
+    grad_prefix = name_pipes(jnp.stack(prefix_grads, axis=0))
     return (output, grad_hidden.reshape(seqs_here, tok_here, model_width), grad_prefix)
 
 

time: 847 us -> 871 us (1.028)
  waiting for transfers between devices: 126 us -> 144 us
  other arithmetic: 101 us -> 113 us
    all_gather x0 -> x1, waiting for transfers between devices: none -> 144 us  [number_zones_for(): return jax.lax.all_gather(a0, peer_axis).sum(axis=0)]
    psum x1 -> x0, waiting for transfers between devices: 126 us -> none  [local(): grad_prefix = lax.psum(jnp.stack(prefix_grads, axis=0), ('rows', 'wide'))]
    reduce_sum x0 -> x1, other arithmetic: none -> 12.8 us  [number_zones_for(): return jax.lax.all_gather(a0, peer_axis).sum(axis=0)]
    unnamed x145 -> x154, local copies, waits for them, and re-layouts: 42.3 us -> 41.9 us
  transfers between devices with their start and end apart: 13 -> 13, of which waited for: 1 -> 1; matrix products, arithmetic and copies ran while one was open for 28% -> 32% of each run, Pallas kernels for 0% -> 0%
where the time goes in v1:
time: 871 us; the launch traced here: 864 us
  matrix products  253 us (29%)
  blocking collectives  167 us (19%)
  waiting for transfers between devices  144 us (17%)
  local copies, waits for them, and re-layouts  142 us (16%)
  other arithmetic  113 us (13%)
  starting transfers between devices  30.5 us (4%)
  between operations  15.5 us (2%)
    all_gather x2, blocking collectives, local(): bias_rows = lax.all_gather(b_up[layer_index], 'wide', axis=0, tiled=True)  167 us
    all_gather x1, waiting for transfers between devices, number_zones_for(): return jax.lax.all_gather(a0, peer_axis).sum(axis=0)  144 us
    dot_general x8, matrix products, multiply(): return jnp.dot(left, right, preferred_element_type=jnp.float32)  86.9 us
    dot_general x6, matrix products, multiply_back(): lax.dot_general(left, right, (((1,), (1,)), ((), ())), preferred_element_...  67.6 us
    unnamed x154, local copies, waits for them, and re-layouts  41.9 us
    concatenate x4, local copies, waits for them, and re-layouts, with_prefix(): return split_heads(jnp.concatenate([fixed_rows, window_part], axis=1))  25.2 us
    ppermute x4, starting transfers between devices, extended(): lax.ppermute(lax.slice_in_dim(block, block.shape[dim] - width, None, axis...  25.2 us
    another operation x4, other arithmetic  24.7 us
  transfers between devices with their start and end apart: 13, of which 1 were waited for; matrix products, arithmetic and copies ran while one was open for 32% of the time, Pallas kernels for 0%

profile of v1, /device:TPU:0, one launch (start us, length us, event | category | flops | bytes accessed | tf_op | source)
XLA Modules:
  0.0 864.4 jit_solution(14200754540990789418)
XLA Ops:
  7.2 3.2 fusion.185
  12.1 6.5 add_convert_fusion.3
  21.5 4.4 collective-permute-start
  28.2 91.8 %all-gather.1 = bf16[1,4096]{1,0:T(2,128)(2,1)S(1)} all-gather(bf16[1,512]{1,0:T(2,128)(2,1)S(1)} %get-tuple-element.47), channel_id=3, replica_groups=mesh['rows'=4,'wide'=8] {'wide'}, dimensions={1}, use_global_device_ids=true | all-gather | bytes 9216 | tf_op jit(solution)/shard_map/all_gather | solution.py:134
  126.4 3.4 pad_maximum_fusion.2
  130.9 3.4 pad_maximum_fusion.4
  134.3 6.1 copy.49
  140.4 6.6 copy.50
  147.1 10.5 %fusion.193 = (f32[4,16,128]{2,1,0:T(8,128)S(1)}, f32[4,16,448,128]{3,2,1,0:T(8,128)}) fusion(bf16[4,448,16,64]{1,3,2,0:T(8,128)(2,1)} %bitcast.216, bf16[4,128,16,64]{1,3,2,0:T(8,128)(2,1)S(1)} %bitcast.225, pred[4,448,128]{2,1,0:T(8,128)(4,1)S(1)} %concatenate.59), kind=kOutput, calls=%fused_computation.264 | convolution fusion | flops 480763904 | bytes 19660800 | tf_op jit(solution)/shard_map/sqhe,skhe->shkq/dot_general | solution.py:104
  157.6 9.0 %fusion = f32[4,16,128]{2,1,0:T(8,128)S(1)} fusion(f32[4,16,448,128]{3,2,1,0:T(8,128)} %get-tuple-element.49, f32[4,16,128]{2,1,0:T(8,128)S(1)} %get-tuple-element.48), kind=kLoop, calls=%fused_computation.18 | loop fusion | flops 7331840 | bytes 14745600 | tf_op jit(solution)/shard_map/reduce_sum | solution.py:121
  166.7 8.5 fusion.134
  178.0 27.0 %fusion.6 = (f32[512,4096]{1,0:T(8,128)}, f32[512,4096]{1,0:T(8,128)}) fusion(f32[4096]{0:T(1024)S(1)} %bitcast.249, bf16[1,4096,1024]{2,1,0:T(8,128)(2,1)} %all-gather.13.cloned.1.call-done, f32[512,1024]{1,0:T(8,128)S(1)} %get-tuple-element.51, f32[1024]{0:T(1024)} %bitcast.274, f32[1024]{0:T(1024)S(1)} %bitcast.261, f32[512]{0:T(512)S(1)} %fusion.163, ...), kind=kOutput, calls=%fused_computation.26 | convolution fusion | flops 4429709312 | bytes 27291648 | tf_op jit(solution)/shard_map/dot_general | solution.py:56
  205.0 12.3 %fusion.195 = (f32[512]{0:T(512)S(1)}, f32[512,1024]{1,0:T(8,128)S(1)}) fusion(f32[1024]{0:T(1024)S(1)} %bitcast.259, bf16[1,4096,1024]{2,1,0:T(8,128)(2,1)} %all-gather.15.cloned.1.call-done, f32[512,4096]{1,0:T(8,128)} %get-tuple-element.52, f32[512,4096]{1,0:T(8,128)} %get-tuple-element.53, f32[4096]{0:T(1024)S(1)} %bitcast.250, ...), kind=kOutput, calls=%fused_computation.266 | convolution fusion | flops 4307025408 | bytes 29394944 | tf_op jit(solution)/shard_map/dot_general | solution.py:52
  217.7 7.0 add_convert_fusion.2
  227.7 4.4 collective-permute-start.2
  232.1 74.9 %all-gather.4 = bf16[1,4096]{1,0:T(2,128)(2,1)S(1)} all-gather(bf16[1,512]{1,0:T(2,128)(2,1)S(1)} %get-tuple-element.46), channel_id=6, replica_groups=mesh['rows'=4,'wide'=8] {'wide'}, dimensions={1}, use_global_device_ids=true | all-gather | bytes 9216 | tf_op jit(solution)/shard_map/all_gather | solution.py:134
  307.1 2.3 slice.245
  311.0 3.8 pad_maximum_fusion.3
  314.8 2.5 fusion.183
  319.6 6.1 copy.54
  325.8 4.1 pad_maximum_fusion.6
  329.9 6.3 copy.53
  336.3 10.6 %fusion.196 = (f32[4,16,128]{2,1,0:T(8,128)S(1)}, f32[4,16,448,128]{3,2,1,0:T(8,128)}) fusion(bf16[4,448,16,64]{1,3,2,0:T(8,128)(2,1)} %bitcast.218, bf16[4,128,16,64]{1,3,2,0:T(8,128)(2,1)S(1)} %bitcast.227, pred[4,448,128]{2,1,0:T(8,128)(4,1)S(1)} %concatenate.59), kind=kOutput, calls=%fused_computation.267 | convolution fusion | flops 480763904 | bytes 19660800 | tf_op jit(solution)/shard_map/sqhe,skhe->shkq/dot_general | solution.py:104
  346.9 9.1 %fusion.1 = f32[4,16,128]{2,1,0:T(8,128)S(1)} fusion(f32[4,16,448,128]{3,2,1,0:T(8,128)} %get-tuple-element.57, f32[4,16,128]{2,1,0:T(8,128)S(1)} %get-tuple-element.56), kind=kLoop, calls=%fused_computation.19 | loop fusion | flops 7331840 | bytes 14745600 | tf_op jit(solution)/shard_map/reduce_sum | solution.py:121
  356.0 8.6 fusion.135
  368.0 26.7 %fusion.7 = (f32[512,4096]{1,0:T(8,128)}, f32[512,4096]{1,0:T(8,128)}) fusion(f32[4096]{0:T(1024)S(1)} %bitcast.252, bf16[1,4096,1024]{2,1,0:T(8,128)(2,1)} %all-gather.17.cloned.1.call-done, f32[512,1024]{1,0:T(8,128)S(1)} %get-tuple-element.59, f32[1024]{0:T(1024)S(1)} %bitcast.270, f32[1024]{0:T(1024)S(1)} %bitcast.267, f32[512]{0:T(512)S(1)} %fusion.165, ...), kind=kOutput, calls=%fused_computation.27 | convolution fusion | flops 4429709312 | bytes 27291648 | tf_op jit(solution)/shard_map/dot_general | solution.py:56
  394.7 11.0 %fusion.198 = (f32[512]{0:T(512)S(1)}, f32[512,1024]{1,0:T(8,128)S(1)}) fusion(f32[1024]{0:T(1024)S(1)} %bitcast.257, bf16[1,4096,1024]{2,1,0:T(8,128)(2,1)} %all-gather.19.cloned.1.call-done, f32[512,4096]{1,0:T(8,128)} %get-tuple-element.60, f32[512,4096]{1,0:T(8,128)} %get-tuple-element.61, f32[4096]{0:T(1024)S(1)} %bitcast.253, ...), kind=kOutput, calls=%fused_computation.269 | convolution fusion | flops 4307025408 | bytes 29394944 | tf_op jit(solution)/shard_map/dot_general | solution.py:52
  406.4 2.6 fusion.180
  409.0 23.4 %multiply_reduce_fusion.4 = (f32[512]{0:T(512)S(1)}, f32[512,1024]{1,0:T(8,128)}) fusion(f32[512,1024]{1,0:T(8,128)S(1)} %get-tuple-element.59, f32[512]{0:T(512)S(1)} %broadcast_multiply_fusion.3, f32[1024]{0:T(1024)S(1)} %bitcast.269, bf16[1,4096,1024]{2,1,0:T(8,128)(2,1)} %all-gather.17.cloned.1.call-done, f32[512,4096]{1,0:T(8,128)} %get-tuple-element.60, ...), kind=kOutput, calls=%fused_computation.153 | convolution fusion | flops 8625586176 | bytes 39872512 | tf_op jit(solution)/shard_map/dot_general | solution.py:52
  432.4 2.3 fusion.179
  440.5 12.0 %fusion.36 = f32[4,16,64,448]{3,2,1,0:T(8,128)} fusion(bf16[4,128,16,64]{1,3,2,0:T(8,128)(2,1)S(1)} %copy.58, f32[4,16,448,128]{3,2,1,0:T(8,128)} %get-tuple-element.57, f32[4,16,128]{2,1,0:T(8,128)S(1)} %log_add_fusion.1), kind=kOutput, calls=%fused_computation.75 | convolution fusion | flops 477102080 | bytes 23101440 | tf_op jit(solution)/shard_map/shkq,sqhe->skhe/dot_general | solution.py:185
  452.5 10.4 %multiply_reduce_fusion.1 = (f32[4,16,128]{2,1,0:T(8,128)S(1)}, f32[4,16,448,128]{3,2,1,0:T(8,128)}) fusion(f32[4,16,448,128]{3,2,1,0:T(8,128)} %get-tuple-element.57, f32[4,16,128]{2,1,0:T(8,128)S(1)} %log_add_fusion.1, bf16[4,448,16,64]{1,3,2,0:T(8,128)(2,1)S(1)} %bitcast.232, bf16[4,128,16,64]{1,3,2,0:T(8,128)(2,1)S(1)} %copy.58), kind=kOutput, calls=%fused_computation.10 | convolution fusion | flops 480763904 | bytes 34144256 | tf_op jit(solution)/shard_map/sqhe,skhe->shkq/dot_general | solution.py:172
  462.9 7.9 slice.247
  470.8 6.6 copy.81
  477.4 10.5 %multiply_convert_fusion.1 = bf16[4,16,448,128]{3,2,1,0:T(8,128)(2,1)S(1)} fusion(f32[4,16,448,128]{3,2,1,0:T(8,128)} %get-tuple-element.67, f32[4,16,448,128]{3,2,1,0:T(8,128)} %get-tuple-element.57, f32[4,16,128]{2,1,0:T(8,128)S(1)} %get-tuple-element.66, f32[4,16,128]{2,1,0:T(8,128)S(1)} %log_add_fusion.1), kind=kLoop, calls=%fused_computation.9 | loop fusion | flops 14680064 | bytes 36765696 | tf_op jit(solution)/shard_map/convert_element_type | solution.py:176
  488.0 3.2 broadcast_multiply_fusion.1
  491.2 3.3 copy-done.2
  494.5 4.3 slice.246
  498.8 6.6 copy.80
  505.4 8.2 fusion.3
  513.7 4.9 fusion.182
  518.6 3.4 collective-permute-start.4
  523.3 4.8 fusion.136
  536.6 4.1 fusion.61
  543.7 3.8 multiply_reduce_fusion.3
  549.5 23.7 %multiply_reduce_fusion.2 = (f32[512]{0:T(512)S(1)}, f32[512,1024]{1,0:T(8,128)}) fusion(f32[512,1024]{1,0:T(8,128)S(1)} %copy-done.15, f32[512]{0:T(512)S(1)} %copy-done.37, f32[1024]{0:T(1024)S(1)} %bitcast.263, bf16[1,4096,1024]{2,1,0:T(8,128)(2,1)} %all-gather.13.cloned.1.call-done, f32[512,4096]{1,0:T(8,128)} %get-tuple-element.52, ...), kind=kOutput, calls=%fused_computation.148 | convolution fusion | flops 8625586176 | bytes 39872512 | tf_op jit(solution)/shard_map/dot_general | solution.py:52
  573.2 2.3 fusion.177
  581.3 11.8 %fusion.34 = f32[4,16,64,448]{3,2,1,0:T(8,128)} fusion(bf16[4,128,16,64]{1,3,2,0:T(8,128)(2,1)S(1)} %copy.65, f32[4,16,448,128]{3,2,1,0:T(8,128)} %get-tuple-element.49, f32[4,16,128]{2,1,0:T(8,128)S(1)} %log_add_fusion), kind=kOutput, calls=%fused_computation.74 | convolution fusion | flops 477102080 | bytes 23101440 | tf_op jit(solution)/shard_map/shkq,sqhe->skhe/dot_general | solution.py:185
  593.2 10.2 %multiply_reduce_fusion = (f32[4,16,128]{2,1,0:T(8,128)S(1)}, f32[4,16,448,128]{3,2,1,0:T(8,128)}) fusion(f32[4,16,448,128]{3,2,1,0:T(8,128)} %get-tuple-element.49, f32[4,16,128]{2,1,0:T(8,128)S(1)} %log_add_fusion, bf16[4,448,16,64]{1,3,2,0:T(8,128)(2,1)S(1)} %bitcast.230, bf16[4,128,16,64]{1,3,2,0:T(8,128)(2,1)S(1)} %copy.65), kind=kOutput, calls=%fused_computation.7 | convolution fusion | flops 480763904 | bytes 34144256 | tf_op jit(solution)/shard_map/sqhe,skhe->shkq/dot_general | solution.py:172
  605.2 10.7 %multiply_convert_fusion = bf16[4,16,448,128]{3,2,1,0:T(8,128)(2,1)S(1)} fusion(f32[4,16,448,128]{3,2,1,0:T(8,128)} %get-tuple-element.73, f32[4,16,448,128]{3,2,1,0:T(8,128)} %get-tuple-element.49, f32[4,16,128]{2,1,0:T(8,128)S(1)} %get-tuple-element.72, f32[4,16,128]{2,1,0:T(8,128)S(1)} %log_add_fusion), kind=kLoop, calls=%fused_computation.6 | loop fusion | flops 14680064 | bytes 36765696 | tf_op jit(solution)/shard_map/convert_element_type | solution.py:176
  615.9 3.2 broadcast_multiply_fusion
  619.2 3.3 copy-done.3
  624.6 7.6 slice.253
  632.2 7.8 slice.252
  640.0 6.9 copy.83
  646.9 6.6 copy.82
  653.5 8.4 fusion.2
  661.8 4.9 fusion.181
  666.8 13.0 %collective-permute-start.6 = (bf16[4,128,2048]{2,1,0:T(8,128)(2,1)}, bf16[4,128,2048]{2,1,0:T(8,128)(2,1)}, u32[]{:S(2)}, u32[]{:S(2)}) collective-permute-start(bf16[4,128,2048]{2,1,0:T(8,128)(2,1)} %get-tuple-element.13), channel_id=1, source_target_pairs={{0,1},{1,2},{2,3},{3,4},{4,5},{5,6},{6,7},{8,9},{9,10},{10,11},{11... | collective-permute-start | bytes 6291464 | tf_op jit(solution)/shard_map/ppermute | solution.py:25
  681.1 4.9 fusion.137
  689.4 4.1 fusion.57
  693.5 7.5 add_add_fusion.8
  701.0 143.7 %all-gather.21.cloned.1.call-done = f32[64,2,64,1024]{3,2,1,0:T(8,128)} async-done(((f32[2,2,64,1024]{3,2,1,0:T(8,128)}), f32[64,2,64,1024]{3,2,1,0:T(8,128)}) %all-gather.21.cloned.1.call-update) | async-done | bytes 33554448 | tf_op jit(solution)/shard_map/all_gather | solution.py:14
  844.7 12.8 %reduce_sum.260 = f32[2,2,64,1024]{3,2,1,0:T(8,128)} reduce(f32[32,2,2,64,1024]{4,3,2,1,0:T(8,128)} %bitcast.220, f32[]{:T(128)} %constant.23.clone.1), dimensions={0}, to_apply=%region_26.27 | reduce | flops 8126464 | bytes 34603012 | tf_op jit(solution)/shard_map/reduce_sum | solution.py:14
  (244 shorter events, 63.0 us)
Async XLA Ops:
  7.2 4.9 copy-start.34
  7.2 4.9 copy-start.70
  7.2 170.7 %all-gather.13.cloned.1.call-start = ((), (), s32[]{:S(2)}) async-start(), calls=%async_computation | async-start | bytes 9437184 | tf_op jit(solution)/shard_map/all_gather | solution.py:132
  10.4 194.5 %all-gather.15.cloned.1.call-start = ((), (), s32[]{:S(2)}) async-start(), calls=%async_computation.1 | async-start | bytes 9437184 | tf_op jit(solution)/shard_map/all_gather | solution.py:133
  12.0 355.9 %all-gather.17.cloned.1.call-start = ((), (), s32[]{:S(2)}) async-start(), calls=%async_computation.2 | async-start | bytes 9437184 | tf_op jit(solution)/shard_map/all_gather | solution.py:132
  18.6 9.6 %copy-start.55 = (bf16[2,512]{1,0:T(2,128)(2,1)S(1)}, bf16[2,512]{1,0:T(2,128)(2,1)}, u32[]{:S(2)}) copy-start(bf16[2,512]{1,0:T(2,128)(2,1)} %param.23) | copy-start | bytes 6148
  18.6 103.1 %copy-start.35 = (s32[4,1024]{1,0:T(4,128)S(1)}, s32[4,1024]{1,0:T(4,128)}, u32[]{:S(2)}) copy-start(s32[4,1024]{1,0:T(4,128)} %param.15) | copy-start | bytes 49156
  18.6 103.4 %copy-start.53 = (f32[2,1024]{1,0:T(2,128)S(1)}, f32[2,1024]{1,0:T(2,128)}, u32[]{:S(2)}) copy-start(f32[2,1024]{1,0:T(2,128)} %param.19) | copy-start | bytes 24580
  18.6 104.0 %copy-start.54 = (f32[2,1024]{1,0:T(2,128)S(1)}, f32[2,1024]{1,0:T(2,128)}, u32[]{:S(2)}) copy-start(f32[2,1024]{1,0:T(2,128)} %param.25) | copy-start | bytes 24580
  18.6 104.6 %copy-start.45 = (f32[2,2,1024]{2,1,0:T(2,128)S(1)}, f32[2,2,1024]{2,1,0:T(2,128)}, u32[]{:S(2)}) copy-start(f32[2,2,1024]{2,1,0:T(2,128)} %param.20) | copy-start | bytes 49156
  18.6 105.2 %copy-start.46 = (f32[2,2,1024]{2,1,0:T(2,128)S(1)}, f32[2,2,1024]{2,1,0:T(2,128)}, u32[]{:S(2)}) copy-start(f32[2,2,1024]{2,1,0:T(2,128)} %param.21) | copy-start | bytes 49156
  20.2 106.2 %collective-permute-start.1 = (bf16[4,128,2048]{2,1,0:T(8,128)(2,1)S(1)}, bf16[4,128,2048]{2,1,0:T(8,128)(2,1)}, u32[]{:S(2)}, u32[]{:S(2)}) collective-permute-start(bf16[4,128,2048]{2,1,0:T(8,128)(2,1)S(1)} %slice.238), channel_id=1, source_target_pairs={{1,0},{2,1},{3,2},{4,3},{5,4},{6,5},{7,6},{9,8},{10,9},{11,10},{12... | collective-permute-start | bytes 6291464 | tf_op jit(solution)/shard_map/ppermute | solution.py:28
  21.5 104.9 %collective-permute-start = (bf16[4,128,2048]{2,1,0:T(8,128)(2,1)S(1)}, bf16[4,128,2048]{2,1,0:T(8,128)(2,1)}, u32[]{:S(2)}, u32[]{:S(2)}) collective-permute-start(bf16[4,128,2048]{2,1,0:T(8,128)(2,1)S(1)} %slice.238), channel_id=1, source_target_pairs={{0,1},{1,2},{2,3},{3,4},{4,5},{5,6},{6,7},{8,9},{9,10},{10,11},{11... | collective-permute-start | bytes 6291464 | tf_op jit(solution)/shard_map/ppermute | solution.py:25
  25.9 368.8 %all-gather.19.cloned.1.call-start = ((), (), s32[]{:S(2)}) async-start(), calls=%async_computation.3 | async-start | bytes 9437184 | tf_op jit(solution)/shard_map/all_gather | solution.py:133
  120.0 84.9 %copy-start.47 = (f32[1,4096]{1,0:T(1,128)}, f32[1,4096]{1,0:T(1,128)S(1)}, u32[]{:S(2)}) copy-start(f32[1,4096]{1,0:T(1,128)S(1)} %convert_element_type.132) | copy-start | bytes 49156
  121.7 25.4 %copy-start.6 = (bf16[4,128,1024]{1,2,0:T(8,128)(2,1)}, bf16[4,128,1024]{1,2,0:T(8,128)(2,1)S(1)}, u32[]{:S(2)}) copy-start(bf16[4,128,1024]{1,2,0:T(8,128)(2,1)S(1)} %copy.51) | copy-start | bytes 3145732
  123.8 81.1 %copy-start.58 = (f32[1,1,1024]{2,1,0:T(1,128)}, f32[1,1,1024]{2,1,0:T(1,128)S(1)}, u32[]{:S(2)}) copy-start(f32[1,1,1024]{2,1,0:T(1,128)S(1)} %get-tuple-element.34) | copy-start | bytes 12292
  123.9 241.6 %copy-start.60 = (f32[1,1,1024]{2,1,0:T(1,128)}, f32[1,1,1024]{2,1,0:T(1,128)S(1)}, u32[]{:S(2)}) copy-start(f32[1,1,1024]{2,1,0:T(1,128)S(1)} %get-tuple-element.33) | copy-start | bytes 12292
  157.6 9.1 %copy-start.29 = (f32[4,16,128]{2,1,0:T(8,128)}, f32[4,16,128]{2,1,0:T(8,128)S(1)}, u32[]{:S(2)}) copy-start(f32[4,16,128]{2,1,0:T(8,128)S(1)} %get-tuple-element.48) | copy-start | bytes 98308
  157.6 9.1 %copy-start.10 = (bf16[4,448,1024]{1,2,0:T(8,128)(2,1)S(1)}, bf16[4,448,1024]{1,2,0:T(8,128)(2,1)}, u32[]{:S(2)}) copy-start(bf16[4,448,1024]{1,2,0:T(8,128)(2,1)} %copy.49) | copy-start | bytes 11010052
  166.6 8.6 copy-start.31
  166.6 9.5 %copy-start.66 = (bf16[2,1024,1024]{2,1,0:T(8,128)(2,1)S(1)}, bf16[2,1024,1024]{2,1,0:T(8,128)(2,1)}, u32[]{:S(2)}) copy-start(bf16[2,1024,1024]{2,1,0:T(8,128)(2,1)} %param.18) | copy-start | bytes 12582916
  166.7 9.5 %copy-start.71 = (bf16[4,128,1024]{2,1,0:T(8,128)(2,1)S(1)}, bf16[4,128,1024]{2,1,0:T(8,128)(2,1)}, u32[]{:S(2)}) copy-start(bf16[4,128,1024]{2,1,0:T(8,128)(2,1)} %param.14) | copy-start | bytes 3145732
  177.5 27.4 %copy-start.14 = (f32[512,1024]{1,0:T(8,128)}, f32[512,1024]{1,0:T(8,128)S(1)}, u32[]{:S(2)}) copy-start(f32[512,1024]{1,0:T(8,128)S(1)} %get-tuple-element.51) | copy-start | bytes 6291460
  177.5 27.4 %copy-start.36 = (f32[512]{0:T(512)}, f32[512]{0:T(512)S(1)}, u32[]{:S(2)}) copy-start(f32[512]{0:T(512)S(1)} %broadcast_multiply_fusion.5) | copy-start | bytes 6148
  177.9 27.0 %copy-start.40 = (f32[512]{0:T(512)}, f32[512]{0:T(512)S(1)}, u32[]{:S(2)}) copy-start(f32[512]{0:T(512)S(1)} %multiply_reduce_fusion.8) | copy-start | bytes 6148
  177.9 27.0 %copy-start.49 = (f32[512]{0:T(512)}, f32[512]{0:T(512)S(1)}, u32[]{:S(2)}) copy-start(f32[512]{0:T(512)S(1)} %fusion.163) | copy-start | bytes 6148
  177.9 27.0 %copy-start.65 = (f32[1,1,1024]{2,1,0:T(1,128)S(1)}, f32[1,1,1024]{2,1,0:T(1,128)}, u32[]{:S(2)}) copy-start(f32[1,1,1024]{2,1,0:T(1,128)} %get-tuple-element.38) | copy-start | bytes 12292
  205.0 12.7 %copy-start.64 = (f32[1,1,1024]{2,1,0:T(1,128)S(1)}, f32[1,1,1024]{2,1,0:T(1,128)}, u32[]{:S(2)}) copy-start(f32[1,1,1024]{2,1,0:T(1,128)} %get-tuple-element.37) | copy-start | bytes 12292
  217.3 7.5 copy-start.16
  217.3 148.2 %copy-start.38 = (f32[512]{0:T(512)}, f32[512]{0:T(512)S(1)}, u32[]{:S(2)}) copy-start(f32[512]{0:T(512)S(1)} %broadcast_multiply_fusion.4) | copy-start | bytes 6148
  217.7 7.1 copy-start.42
  217.7 147.8 %copy-start.51 = (f32[512]{0:T(512)}, f32[512]{0:T(512)S(1)}, u32[]{:S(2)}) copy-start(f32[512]{0:T(512)S(1)} %fusion.164) | copy-start | bytes 6148
  226.4 84.6 %collective-permute-start.3 = (bf16[4,128,2048]{2,1,0:T(8,128)(2,1)S(1)}, bf16[4,128,2048]{2,1,0:T(8,128)(2,1)}, u32[]{:S(2)}, u32[]{:S(2)}) collective-permute-start(bf16[4,128,2048]{2,1,0:T(8,128)(2,1)S(1)} %slice.242), channel_id=1, source_target_pairs={{1,0},{2,1},{3,2},{4,3},{5,4},{6,5},{7,6},{9,8},{10,9},{11,10},{12... | collective-permute-start | bytes 6291464 | tf_op jit(solution)/shard_map/ppermute | solution.py:28
  227.7 83.3 %collective-permute-start.2 = (bf16[4,128,2048]{2,1,0:T(8,128)(2,1)S(1)}, bf16[4,128,2048]{2,1,0:T(8,128)(2,1)}, u32[]{:S(2)}, u32[]{:S(2)}) collective-permute-start(bf16[4,128,2048]{2,1,0:T(8,128)(2,1)S(1)} %slice.242), channel_id=1, source_target_pairs={{0,1},{1,2},{2,3},{3,4},{4,5},{5,6},{6,7},{8,9},{9,10},{10,11},{11... | collective-permute-start | bytes 6291464 | tf_op jit(solution)/shard_map/ppermute | solution.py:25
  232.1 612.7 %all-gather.21.cloned.1.call-start = ((), (), s32[]{:S(2)}) async-start(), calls=%async_computation.4 | async-start | bytes 34603008 | tf_op jit(solution)/shard_map/all_gather | solution.py:14
  311.0 25.3 %copy-start.8 = (bf16[4,128,1024]{1,2,0:T(8,128)(2,1)}, bf16[4,128,1024]{1,2,0:T(8,128)(2,1)S(1)}, u32[]{:S(2)}) copy-start(bf16[4,128,1024]{1,2,0:T(8,128)(2,1)S(1)} %copy.55) | copy-start | bytes 3145732
  346.9 9.1 %copy-start.12 = (bf16[4,448,1024]{1,2,0:T(8,128)(2,1)S(1)}, bf16[4,448,1024]{1,2,0:T(8,128)(2,1)}, u32[]{:S(2)}) copy-start(bf16[4,448,1024]{1,2,0:T(8,128)(2,1)} %copy.53) | copy-start | bytes 11010052
  355.9 9.5 %copy-start.17 = (f32[512,1024]{1,0:T(8,128)S(1)}, f32[512,1024]{1,0:T(8,128)}, u32[]{:S(2)}) copy-start(f32[512,1024]{1,0:T(8,128)} %copy-done.16) | copy-start | bytes 6291460
  356.0 9.5 %copy-start.57 = (f32[1,1024]{1,0:T(1,128)S(1)}, f32[1,1024]{1,0:T(1,128)}, u32[]{:S(2)}) copy-start(f32[1,1024]{1,0:T(1,128)} %get-tuple-element.42) | copy-start | bytes 12292
  356.0 9.5 %copy-start.67 = (bf16[2,1024,1024]{2,1,0:T(8,128)(2,1)S(1)}, bf16[2,1024,1024]{2,1,0:T(8,128)(2,1)}, u32[]{:S(2)}) copy-start(bf16[2,1024,1024]{2,1,0:T(8,128)(2,1)} %param.18) | copy-start | bytes 12582916
  368.0 26.7 %copy-start.56 = (f32[1,1024]{1,0:T(1,128)S(1)}, f32[1,1024]{1,0:T(1,128)}, u32[]{:S(2)}) copy-start(f32[1,1024]{1,0:T(1,128)} %get-tuple-element.40) | copy-start | bytes 12292
  394.7 11.1 %copy-start.20 = (bf16[4,128,1024]{2,1,0:T(8,128)(2,1)S(1)}, bf16[4,128,1024]{2,1,0:T(8,128)(2,1)}, u32[]{:S(2)}) copy-start(bf16[4,128,1024]{2,1,0:T(8,128)(2,1)} %param.27) | copy-start | bytes 3145732
  394.7 11.1 %copy-start.33 = (f32[1,1,1024]{2,1,0:T(1,128)S(1)}, f32[1,1,1024]{2,1,0:T(1,128)}, u32[]{:S(2)}) copy-start(f32[1,1,1024]{2,1,0:T(1,128)} %get-tuple-element.32) | copy-start | bytes 12292
  394.7 11.7 %copy-start.44 = (f32[1,1,1024]{2,1,0:T(1,128)S(1)}, f32[1,1,1024]{2,1,0:T(1,128)}, u32[]{:S(2)}) copy-start(f32[1,1,1024]{2,1,0:T(1,128)} %get-tuple-element.36) | copy-start | bytes 12292
  440.5 12.0 %copy-start.13 = (bf16[4,448,1024]{1,2,0:T(8,128)(2,1)S(1)}, bf16[4,448,1024]{1,2,0:T(8,128)(2,1)}, u32[]{:S(2)}) copy-start(bf16[4,448,1024]{1,2,0:T(8,128)(2,1)} %copy.53) | copy-start | bytes 11010052
  477.4 10.5 %copy-start.9 = (bf16[4,128,1024]{1,2,0:T(8,128)(2,1)S(1)}, bf16[4,128,1024]{1,2,0:T(8,128)(2,1)}, u32[]{:S(2)}) copy-start(bf16[4,128,1024]{1,2,0:T(8,128)(2,1)} %copy-done.8) | copy-start | bytes 3145732
  513.7 9.6 %copy-start.30 = (f32[4,16,128]{2,1,0:T(8,128)S(1)}, f32[4,16,128]{2,1,0:T(8,128)}, u32[]{:S(2)}) copy-start(f32[4,16,128]{2,1,0:T(8,128)} %copy-done.29) | copy-start | bytes 98308
  513.7 9.6 %copy-start.32 = (f32[4,16,128]{2,1,0:T(8,128)S(1)}, f32[4,16,128]{2,1,0:T(8,128)}, u32[]{:S(2)}) copy-start(f32[4,16,128]{2,1,0:T(8,128)} %copy-done.31) | copy-start | bytes 98308
  513.7 9.7 %copy-start.5 = (bf16[4,448,1024]{1,2,0:T(8,128)(2,1)S(1)}, bf16[4,448,1024]{1,2,0:T(8,128)(2,1)}, u32[]{:S(2)}) copy-start(bf16[4,448,1024]{1,2,0:T(8,128)(2,1)} %copy.54) | copy-start | bytes 11010052
  518.6 18.0 %collective-permute-start.4 = (bf16[4,128,2048]{2,1,0:T(8,128)(2,1)}, bf16[4,128,2048]{2,1,0:T(8,128)(2,1)}, u32[]{:S(2)}, u32[]{:S(2)}) collective-permute-start(bf16[4,128,2048]{2,1,0:T(8,128)(2,1)} %get-tuple-element.15), channel_id=1, source_target_pairs={{0,1},{1,2},{2,3},{3,4},{4,5},{5,6},{6,7},{8,9},{9,10},{10,11},{11... | collective-permute-start | bytes 6291464 | tf_op jit(solution)/shard_map/ppermute | solution.py:25
  522.0 14.6 %collective-permute-start.5 = (bf16[4,128,2048]{2,1,0:T(8,128)(2,1)}, bf16[4,128,2048]{2,1,0:T(8,128)(2,1)}, u32[]{:S(2)}, u32[]{:S(2)}) collective-permute-start(bf16[4,128,2048]{2,1,0:T(8,128)(2,1)} %get-tuple-element.16), channel_id=1, source_target_pairs={{1,0},{2,1},{3,2},{4,3},{5,4},{6,5},{7,6},{9,8},{10,9},{11,10},{12... | collective-permute-start | bytes 6291464 | tf_op jit(solution)/shard_map/ppermute | solution.py:28
  531.8 8.9 %slice-start = ((s8[12582912]{0:T(1024)(128)(4,1)}), s8[4194304]{0:T(1024)(128)(4,1)S(1)}, s32[]{:S(2)}) async-start(s8[12582912]{0:T(1024)(128)(4,1)} %bitcast.276), calls=%async_computation.5 | async-start | bytes 8388608
  536.6 4.7 copy-start.61
  536.6 5.9 slice-start.1
  536.6 7.1 slice-start.2
  549.5 23.8 %copy-start.41 = (f32[512]{0:T(512)S(1)}, f32[512]{0:T(512)}, u32[]{:S(2)}) copy-start(f32[512]{0:T(512)} %copy-done.40) | copy-start | bytes 6148
  549.5 23.8 %copy-start.50 = (f32[512]{0:T(512)S(1)}, f32[512]{0:T(512)}, u32[]{:S(2)}) copy-start(f32[512]{0:T(512)} %copy-done.49) | copy-start | bytes 6148
  581.3 11.8 %copy-start.11 = (bf16[4,448,1024]{1,2,0:T(8,128)(2,1)S(1)}, bf16[4,448,1024]{1,2,0:T(8,128)(2,1)}, u32[]{:S(2)}) copy-start(bf16[4,448,1024]{1,2,0:T(8,128)(2,1)} %copy.49) | copy-start | bytes 11010052
  605.1 10.8 %copy-start.7 = (bf16[4,128,1024]{1,2,0:T(8,128)(2,1)S(1)}, bf16[4,128,1024]{1,2,0:T(8,128)(2,1)}, u32[]{:S(2)}) copy-start(bf16[4,128,1024]{1,2,0:T(8,128)(2,1)} %copy-done.6) | copy-start | bytes 3145732
  615.9 6.9 copy-start.19
  661.8 19.2 %copy-start.4 = (bf16[4,448,1024]{1,2,0:T(8,128)(2,1)S(1)}, bf16[4,448,1024]{1,2,0:T(8,128)(2,1)}, u32[]{:S(2)}) copy-start(bf16[4,448,1024]{1,2,0:T(8,128)(2,1)} %copy.50) | copy-start | bytes 11010052
  666.8 22.6 %collective-permute-start.6 = (bf16[4,128,2048]{2,1,0:T(8,128)(2,1)}, bf16[4,128,2048]{2,1,0:T(8,128)(2,1)}, u32[]{:S(2)}, u32[]{:S(2)}) collective-permute-start(bf16[4,128,2048]{2,1,0:T(8,128)(2,1)} %get-tuple-element.13), channel_id=1, source_target_pairs={{0,1},{1,2},{2,3},{3,4},{4,5},{5,6},{6,7},{8,9},{9,10},{10,11},{11... | collective-permute-start | bytes 6291464 | tf_op jit(solution)/shard_map/ppermute | solution.py:25
  679.8 9.6 %collective-permute-start.7 = (bf16[4,128,2048]{2,1,0:T(8,128)(2,1)}, bf16[4,128,2048]{2,1,0:T(8,128)(2,1)}, u32[]{:S(2)}, u32[]{:S(2)}) collective-permute-start(bf16[4,128,2048]{2,1,0:T(8,128)(2,1)} %get-tuple-element.14), channel_id=1, source_target_pairs={{1,0},{2,1},{3,2},{4,3},{5,4},{6,5},{7,6},{9,8},{10,9},{11,10},{12... | collective-permute-start | bytes 6291464 | tf_op jit(solution)/shard_map/ppermute | solution.py:28
  (24 other events, 70.1 us)
Sparse Core Ops, SparseCore 0:
  10.6 101.7 all-gather.12
  114.6 85.6 all-gather.14
  201.9 97.0 all-gather.16
  301.0 86.1 all-gather.18
  624.7 219.9 all-gather.20
